TPU v7x, 32 devices: a whole 2x2x4 slice. The times are simulated.
32 devices in a mesh: parts: 2 (over y), row: 16 (over z, x, core).
Axes of the slice: x: 2, y: 2, z: 4, core: 2. Of those that a mesh axis runs over, the one named last changes fastest.
Arguments:
- object_tile: float32 [2, 8192, 256], P(None, ('parts', 'row')), parts along dimension 1, may hold values from -6 to 6
- probe_modes: float32 [2, 4, 128, 128], replicated, may hold values from -4 to 4
- measured: float32 [128, 128, 128], P(('parts', 'row')), parts along dimension 0, may hold values from 0.5 to 8
- offsets: int32 [128, 2], P(('parts', 'row')), parts along dimension 0, may hold values from -64 to 192, as said below
- counts: int32 [32], P(('parts', 'row')), parts along dimension 0, may hold values from 2 to 4, as said below
Outputs:
- object_out: float32 [2, 8192, 256], P(None, ('parts', 'row')), parts along dimension 1
- probe_out: float32 [4, 4, 128, 128], P('parts'), parts along dimension 0
There are 2 independent parts, one for each index of `parts`. A program takes and returns all parts, laid end to end along the dimension named above; an argument that names none is the same for every part. Nothing has to cross between parts.
Inputs may be any that keep to these rules, and one draw needn't show every extreme that they name: `offsets`: column 0 is a row offset relative to the tile's first row, from -64 to 192; in every tile the first slot has -64 and the second 256 - 64; column 1 is a column offset from 0 to 128. counts[t] live slots of tile t come first, the others are unused; some tile has 4.
All inputs are finite; a program needn't handle non-finite values.
Results may differ from a plain program's by a relative error of at most 0.0003.
Values sent between devices are 32-bit elements; how exact they have to be, the bound alone decides.
A program may use at most 64 MiB of HBM per device.

v0:
```python
import functools
import math

import jax
import jax.numpy as jnp
import numpy as np
from jax import lax
from jax.experimental import pallas as pl
from jax.experimental.pallas import tpu as pltpu
from jax.sharding import PartitionSpec as P

ITERS = 2
object_rate = 0.2
probe_rate = 0.5
ENERGY_ROWS = 8
VMEM = pl.BlockSpec(memory_space=pltpu.VMEM)
ANY = pl.BlockSpec(memory_space=pl.ANY)
SMEM = pl.BlockSpec(memory_space=pltpu.SMEM)
MESH = pl.DeviceIdType.MESH


def dft_tables(length):
    index = np.arange(length)
    phase = 2.0 * math.pi / length * (index[:, None] * index[None, :] % length)
    cosine = np.cos(phase) / math.sqrt(length)
    sine = -np.sin(phase) / math.sqrt(length)
    forward = np.block([[cosine, -sine], [sine, cosine]]).astype(np.float32)
    backward = np.block([[cosine, sine], [-sine, cosine]]).astype(np.float32)
    tables = []
    for table in (forward, backward):
        high = table.astype(jnp.bfloat16)
        low = (table - high.astype(np.float32)).astype(jnp.bfloat16)
        tables.append(jnp.asarray(np.concatenate([high, high, low], axis=1)))
        tables.append(jnp.asarray(np.concatenate([high, high, low], axis=0)))
    return tables


def halves(x):
    high = x.astype(jnp.bfloat16)
    return high, (x - high.astype(jnp.float32)).astype(jnp.bfloat16)


def gradient_kernel(
    offsets, counts, obj, probe, measured, left_f, right_f, left_b, right_b,
    grad, probe_grad, x3, y3, far, columns, sums,
):
    slots, length = measured.shape[0], measured.shape[1]
    modes = probe.shape[1]
    cols = obj.shape[2]
    margin = length // 2
    half = modes * length
    blocks = range(cols // length)
    for c in range(obj.shape[0]):
        for j in blocks:
            columns[c, j] = obj[c, :, j * length : (j + 1) * length]
    sums[...] = jnp.zeros_like(sums)
    probe_grad[...] = jnp.zeros_like(probe_grad)
    wide = 2 * length

    def put_x(k, part, value):
        high, low = halves(value)
        c = pl.ds(k * length, length)
        x3[pl.ds(part * length, length), c] = high
        x3[pl.ds(wide + part * length, length), c] = low
        x3[pl.ds(2 * wide + part * length, length), c] = high

    def put_y(k, part, value):
        high, low = halves(value)
        r = pl.ds(k * length, length)
        y3[r, pl.ds(part * length, length)] = high
        y3[r, pl.ds(wide + part * length, length)] = low
        y3[r, pl.ds(2 * wide + part * length, length)] = high

    def visit(s, carry):
        row = offsets[0, s] + margin
        col = offsets[1, s]
        shift = lax.rem(cols - col, cols)

        def cut(c):
            whole = jnp.concatenate([columns[c, j, pl.ds(row, length), :] for j in blocks], axis=1)
            return pltpu.roll(whole, shift, 1)[:, :length]

        wr, wi = cut(0), cut(1)
        energy = (wr * wr + wi * wi).reshape(-1, ENERGY_ROWS, length).sum(axis=0)
        probe_grad[0, half:, :] += energy
        probe_grad[1, half:, :] += energy
        for k in range(modes):
            pr, pi = probe[0, k], probe[1, k]
            put_x(k, 0, pr * wr - pi * wi)
            put_x(k, 1, pr * wi + pi * wr)
        left = jnp.dot(left_f[...], x3[...], preferred_element_type=jnp.float32)
        for k in range(modes):
            for part in range(2):
                put_y(k, part, left[part * length : (part + 1) * length, k * length : (k + 1) * length])
        far[...] = jnp.dot(y3[...], right_f[...], preferred_element_type=jnp.float32)
        intensity = jnp.zeros((length, length), jnp.float32)
        for k in range(modes):
            fr = far[k * length : (k + 1) * length, :length]
            fi = far[k * length : (k + 1) * length, length:]
            intensity = intensity + (fr * fr + fi * fi)
        resid = intensity - measured[s]
        for k in range(modes):
            for part in range(2):
                put_y(
                    k, part,
                    resid * far[k * length : (k + 1) * length, part * length : (part + 1) * length],
                )
        right = jnp.dot(y3[...], right_b[...], preferred_element_type=jnp.float32)
        for k in range(modes):
            for part in range(2):
                put_x(k, part, right[k * length : (k + 1) * length, part * length : (part + 1) * length])
        back = jnp.dot(left_b[...], x3[...], preferred_element_type=jnp.float32)
        gr = jnp.zeros((length, length), jnp.float32)
        gi = jnp.zeros((length, length), jnp.float32)
        wr, wi = cut(0), cut(1)
        for k in range(modes):
            pr, pi = probe[0, k], probe[1, k]
            br = back[:length, k * length : (k + 1) * length]
            bi = back[length:, k * length : (k + 1) * length]
            gr = gr + (pr * br + pi * bi)
            gi = gi + (pr * bi - pi * br)
            probe_grad[0, k * length : (k + 1) * length, :] += wr * br + wi * bi
            probe_grad[1, k * length : (k + 1) * length, :] += wr * bi - wi * br
        rest = jnp.zeros((length, cols - length), jnp.float32)
        for c, g in ((0, gr), (1, gi)):
            placed = pltpu.roll(jnp.concatenate([g, rest], axis=1), col, 1)
            for j in blocks:
                sums[c, j, pl.ds(row, length), :] += placed[:, j * length : (j + 1) * length]
        return carry

    lax.fori_loop(0, jnp.minimum(counts[0], slots), visit, 0)
    for c in range(obj.shape[0]):
        for j in blocks:
            grad[c, :, j * length : (j + 1) * length] = sums[c, j]


def greet(me, n, devices):
    barrier = pltpu.get_barrier_semaphore()

    def signal(device):
        pl.semaphore_signal(barrier, inc=1, device_id={"row": device}, device_id_type=MESH)

    pl.when(me > 0)(lambda: signal(me - 1))
    pl.when(me < n - 1)(lambda: signal(me + 1))
    for device in devices:
        signal(device)
    inside = (me > 0) & (me < n - 1)
    pl.when(inside)(lambda: pl.semaphore_wait(barrier, len(devices) + 2))
    pl.when(jnp.logical_not(inside))(lambda: pl.semaphore_wait(barrier, len(devices) + 1))


def remote(src, dst, send, recv, device):
    return pltpu.make_async_remote_copy(
        src_ref=src, dst_ref=dst, send_sem=send, recv_sem=recv,
        device_id={"row": device}, device_id_type=MESH,
    )


def exchange(me, n, array, rows_up, rows_down, from_up, from_down, sems):
    up = remote(array.at[:, rows_up], from_down, sems.at[0], sems.at[1], me - 1)
    down = remote(array.at[:, rows_down], from_up, sems.at[2], sems.at[3], me + 1)

    def start():
        pl.when(me > 0)(up.start)
        pl.when(me < n - 1)(down.start)

    def wait():
        @pl.when(me > 0)
        def _():
            up.wait_send()
            down.wait_recv()

        @pl.when(me < n - 1)
        def _():
            down.wait_send()
            up.wait_recv()

    return start, wait


def halo_kernel(n, tile, padded, from_up, from_down, sems):
    me = lax.axis_index("row")
    rows = tile.shape[1]
    margin = from_up.shape[1]
    greet(me, n, [])
    start, wait = exchange(
        me, n, tile, pl.ds(0, margin), pl.ds(rows - margin, margin), from_up, from_down, sems
    )
    start()
    padded[:, margin : margin + rows] = tile[...]

    @pl.when(me == 0)
    def _():
        padded[:, :margin] = jnp.zeros_like(from_up)

    @pl.when(me == n - 1)
    def _():
        padded[:, margin + rows :] = jnp.zeros_like(from_down)

    wait()

    @pl.when(me > 0)
    def _():
        padded[:, :margin] = from_up[...]

    @pl.when(me < n - 1)
    def _():
        padded[:, margin + rows :] = from_down[...]


def update_kernel(
    n, final, modes, obj_in, grad_in, probe_in, probe_grad, new_obj, new_probe,
    from_up, from_down, obj, grad, made, probe, r1, t2, r2, t3, r3, fresh,
    local_sems, edge_sems, pair_sems, out2, in2,
    out3, in3, gout3, gin3, gout2, gin2, gout1, gin1,
):
    me = lax.axis_index("row")
    length = probe.shape[1]
    margin = length // 2
    padded_rows = obj.shape[1]
    edge = from_up.shape[1]
    peers = t3.shape[0]
    rows = t3.shape[1] - ENERGY_ROWS
    half, quarter = probe.shape[0] // 2, probe.shape[0] // 4
    core = me % 2
    second = (me // 2) % 2
    rank = me // 4
    mate = me + 1 - 2 * core
    other = me + 2 - 4 * second
    ranks = [(rank + d) % peers for d in range(1, peers)]
    loads = [
        pltpu.make_async_copy(src, dst, local_sems.at[i])
        for i, (src, dst) in enumerate(((probe_in, probe), (obj_in, obj), (grad_in, grad)))
    ]
    for load in loads:
        load.start()
    greet(me, n, [mate, other] + [p * 4 + me % 4 for p in ranks])
    one = remote(probe_grad.at[1 - core], r1, pair_sems.at[0], pair_sems.at[1], mate)
    one.start()

    @pl.when(me == 0)
    def _():
        from_up[...] = jnp.zeros_like(from_up)

    @pl.when(me == n - 1)
    def _():
        from_down[...] = jnp.zeros_like(from_down)

    one.wait_recv()

    def add_pair(b, p):
        part = pl.ds(pl.multiple_of(b * quarter + p * rows, rows), rows)
        t2[b, p, :rows] = probe_grad[core, part] + r1[part]
        t2[b, p, rows:] = probe_grad[core, half:] + r1[half:]

    sends = [one]

    def pass_on(copy):
        copy.start()
        sends.append(copy)

    def to_second(p):
        return remote(t2.at[1 - second, p], r2.at[p], out2.at[p], in2.at[p], other)

    for p in ranks + [rank]:
        add_pair(1 - second, p)
        pass_on(to_second(p))
    start, wait = exchange(
        me, n, grad_in, pl.ds(0, edge), pl.ds(padded_rows - edge, edge), from_up, from_down, edge_sems
    )
    start()
    for p in ranks + [rank]:
        add_pair(second, p)
    for p in ranks + [rank]:
        to_second(p).wait_recv()
        t3[p] = t2[second, p] + r2[p]
        if p is not rank:
            pass_on(remote(t3.at[p], r3.at[rank], out3.at[p], in3.at[rank], p * 4 + me % 4))

    loads[0].wait()
    power = jnp.zeros((length, length), jnp.float32)
    for k in range(2 * modes):
        p = probe[k * length : (k + 1) * length, :]
        power = power + p * p
    step = object_rate / jnp.max(power, axis=(0, 1), keepdims=True)
    loads[1].wait()
    loads[2].wait()
    base = margin if final else 0

    def out(s):
        return slice(s.start - base, s.stop - base)

    inner = slice(base + edge, padded_rows - base - edge)
    top = slice(base, base + edge)
    low = slice(padded_rows - base - edge, padded_rows - base)
    made[:, out(inner)] = obj[:, inner] - step * grad[:, inner]

    share = t3[rank]
    for p in ranks:
        remote(t3.at[p], r3.at[p], out3.at[p], in3.at[p], p * 4 + me % 4).wait_recv()
        share = share + r3[p]
    energy = jnp.sum(share[rows:], axis=(0, 1), keepdims=True)

    def region(c, b, p):
        return pl.ds(pl.multiple_of(c * half + b * quarter + p * rows, rows), rows)

    own = region(core, second, rank)
    fresh[own, :] = probe[own, :] - probe_rate * length * length / energy * share[:rows]

    def to_rank(p, q):
        part = fresh.at[region(core, second, q)]
        return remote(part, part, gout3.at[p], gin3.at[q], p * 4 + me % 4)

    def to_other(b, p):
        part = fresh.at[region(core, b, p)]
        return remote(part, part, gout2.at[p], gin2.at[p], other)

    def to_mate(c, b, p):
        part = fresh.at[region(c, b, p)]
        return remote(part, part, gout1.at[b * peers + p], gin1.at[b * peers + p], mate)

    for p in ranks:
        pass_on(to_rank(p, rank))
    pass_on(to_other(second, rank))
    pass_on(to_mate(core, second, rank))
    for p in ranks:
        to_rank(p, p).wait_recv()
        pass_on(to_other(second, p))
        pass_on(to_mate(core, second, p))

    wait()
    made[:, out(top)] = obj[:, top] - step * (grad[:, top] + from_up[...])
    made[:, out(low)] = obj[:, low] - step * (grad[:, low] + from_down[...])
    if not final:
        @pl.when(me == 0)
        def _():
            made[:, :margin] = jnp.zeros((2, margin, obj.shape[2]), jnp.float32)

        @pl.when(me == n - 1)
        def _():
            made[:, padded_rows - margin :] = jnp.zeros((2, margin, obj.shape[2]), jnp.float32)

    store = pltpu.make_async_copy(made, new_obj, local_sems.at[1])
    store.start()
    for p in [rank] + ranks:
        to_other(1 - second, p).wait_recv()
        pass_on(to_mate(core, 1 - second, p))
    for p in [rank] + ranks:
        to_mate(1 - core, second, p).wait_recv()
    for p in [rank] + ranks:
        to_mate(1 - core, 1 - second, p).wait_recv()
    result = pltpu.make_async_copy(fresh, new_probe, local_sems.at[0])
    result.start()
    for copy in sends:
        copy.wait_send()
    store.wait()
    result.wait()


def body(object_tile, probe_modes, measured, offsets, counts):
    n = lax.axis_size("row")
    parts, tile_rows, cols = object_tile.shape
    modes, length = probe_modes.shape[1], probe_modes.shape[2]
    margin = length // 2
    padded_rows = tile_rows + 2 * margin
    flat = 2 * modes * length
    half, quarter = flat // 2, flat // 4
    peers = n // 4
    rows = quarter // peers
    f32 = jnp.float32
    dma = pltpu.SemaphoreType.DMA
    padded_shape = jax.ShapeDtypeStruct((parts, padded_rows, cols), f32)
    tables = dft_tables(length)

    padded = pl.pallas_call(
        functools.partial(halo_kernel, n),
        name="halo",
        out_shape=padded_shape,
        in_specs=[VMEM],
        out_specs=VMEM,
        scratch_shapes=[pltpu.VMEM((parts, margin, cols), f32)] * 2 + [dma((4,))],
        compiler_params=pltpu.CompilerParams(collective_id=0, has_side_effects=True),
    )(object_tile)

    gradient = pl.pallas_call(
        gradient_kernel,
        name="gradient",
        out_shape=[padded_shape, jax.ShapeDtypeStruct((2, half + ENERGY_ROWS, length), f32)],
        in_specs=[SMEM, SMEM] + [VMEM] * 7,
        out_specs=[VMEM, VMEM],
        scratch_shapes=[
            pltpu.VMEM((6 * length, modes * length), jnp.bfloat16),
            pltpu.VMEM((modes * length, 6 * length), jnp.bfloat16),
            pltpu.VMEM((modes * length, 2 * length), f32),
        ]
        + [pltpu.VMEM((parts, cols // length, padded_rows, length), f32)] * 2,
    )

    probe_now = probe_modes
    for sweep in range(ITERS):
        final = sweep == ITERS - 1
        edge = margin if final else 2 * margin
        grad, probe_grad = gradient(
            offsets.T, counts, padded, probe_now, measured, tables[0], tables[3], tables[2], tables[1]
        )
        padded, fresh = pl.pallas_call(
            functools.partial(update_kernel, n, final, modes),
            name="update_last" if final else "update",
            out_shape=[
                jax.ShapeDtypeStruct((parts, tile_rows if final else padded_rows, cols), f32),
                jax.ShapeDtypeStruct((flat, length), f32),
            ],
            in_specs=[ANY] * 3 + [VMEM],
            out_specs=[ANY] * 2,
            scratch_shapes=[
                pltpu.VMEM((parts, edge, cols), f32),
                pltpu.VMEM((parts, edge, cols), f32),
                pltpu.VMEM((parts, padded_rows, cols), f32),
                pltpu.VMEM((parts, padded_rows, cols), f32),
                pltpu.VMEM((parts, tile_rows if final else padded_rows, cols), f32),
                pltpu.VMEM((flat, length), f32),
                pltpu.VMEM((half + ENERGY_ROWS, length), f32),
                pltpu.VMEM((2, peers, rows + ENERGY_ROWS, length), f32),
                pltpu.VMEM((peers, rows + ENERGY_ROWS, length), f32),
                pltpu.VMEM((peers, rows + ENERGY_ROWS, length), f32),
                pltpu.VMEM((peers, rows + ENERGY_ROWS, length), f32),
                pltpu.VMEM((flat, length), f32),
                dma((3,)),
                dma((4,)),
                dma((2,)),
                dma((peers,)), dma((peers,)),
                dma((peers,)), dma((peers,)), dma((peers,)), dma((peers,)),
                dma((peers,)), dma((peers,)), dma((2 * peers,)), dma((2 * peers,)),
            ],
            compiler_params=pltpu.CompilerParams(
                collective_id=1 + sweep, has_side_effects=True
            ),
        )(padded, grad, probe_now.reshape(flat, length), probe_grad)
        probe_now = fresh.reshape(probe_modes.shape)
    return (padded, probe_now)


def solution(mesh):
    return jax.shard_map(
        body,
        mesh=mesh,
        in_specs=(
            P(None, ("parts", "row"), None),
            P(),
            P(("parts", "row"), None, None),
            P(("parts", "row"), None),
            P(("parts", "row")),
        ),
        out_specs=(P(None, ("parts", "row"), None), P("parts", None, None, None)),
        check_vma=False,
    )
```

profile of v0, /device:TPU:0, one launch (start us, length us, event | category | flops | bytes accessed | tf_op | source)
XLA Modules:
  0.0 84.1 jit_solution(16316149389742517063)
XLA Ops:
  1.3 5.9 %halo.1.obj.obj_in = f32[2,384,256]{2,1,0:T(8,128)} custom-call(f32[2,256,256]{2,1,0:T(8,128)} %tile.1), custom_call_target="tpu_custom_call" | custom-call | tf_op jit(solution)/shard_map/halo/pallas_call | solution.py:375
  7.2 7.5 %gradient.2 = (f32[2,384,256]{2,1,0:T(8,128)}, f32[2,520,128]{2,1,0:T(8,128)}) custom-call(s32[2,4]{1,0:T(2,128)} %bitcast.7, s32[1]{0:T(128)S(6)} %copy.13.counts, f32[2,384,256]{2,1,0:T(8,128)} %halo.1.obj.obj_in, f32[2,4,128,128]{3,2,1,0:T(8,128)} %probe.1, f32[4,128,128]{2,1,0:T(8,128)} %measured.3, bf16[256,768]{1,0:T(8,128)(2,1)} %constant.8.clone.left_f, ...), custom_call_target="tpu_custom_call" | custom-call | tf_op jit(solution)/shard_map/gradient/pallas_call | solution.py:403
  14.7 31.5 %update.1 = (f32[2,384,256]{2,1,0:T(8,128)}, f32[1024,128]{1,0:T(8,128)}) custom-call(f32[2,384,256]{2,1,0:T(8,128)} %halo.1.obj.obj_in, f32[2,384,256]{2,1,0:T(8,128)} %get-tuple-element.10.grad_in, f32[1024,128]{1,0:T(8,128)} %bitcast.4, f32[2,520,128]{2,1,0:T(8,128)} %get-tuple-element.11.probe_grad), custom_call_target="tpu_custom_call" | custom-call | tf_op jit(solution)/shard_map/update/pallas_call | solution.py:406
  46.3 7.6 %gradient.3 = (f32[2,384,256]{2,1,0:T(8,128)}, f32[2,520,128]{2,1,0:T(8,128)}) custom-call(s32[2,4]{1,0:T(2,128)} %bitcast.8, s32[1]{0:T(128)S(6)} %copy.13.counts, f32[2,384,256]{2,1,0:T(8,128)} %get-tuple-element.12.obj.obj_in, f32[2,4,128,128]{3,2,1,0:T(8,128)} %bitcast.5, f32[4,128,128]{2,1,0:T(8,128)} %measured.3, ...), custom_call_target="tpu_custom_call" | custom-call | tf_op jit(solution)/shard_map/gradient/pallas_call | solution.py:403
  53.9 27.5 %update_last.1 = (f32[2,256,256]{2,1,0:T(8,128)}, f32[1024,128]{1,0:T(8,128)}) custom-call(f32[2,384,256]{2,1,0:T(8,128)} %get-tuple-element.12.obj.obj_in, f32[2,384,256]{2,1,0:T(8,128)} %get-tuple-element.14.grad_in, f32[1024,128]{1,0:T(8,128)} %get-tuple-element.13.probe_in, f32[2,520,128]{2,1,0:T(8,128)} %get-tuple-element.15.probe_grad), custom_call_target="tpu_custom_call" | custom-call | tf_op jit(solution)/shard_map/update_last/pallas_call | solution.py:406
  81.4 0.0 copy-start
  81.4 1.9 %copy.14 = f32[2,256,256]{2,1,0:T(8,128)} copy(f32[2,256,256]{2,1,0:T(8,128)} %get-tuple-element.20) | data formatting | bytes 1048576
  83.3 0.0 copy-done
  83.3 0.8 copy.15
Async XLA Ops:
  81.4 1.9 %copy-start = (f32[1024,128]{1,0:T(8,128)S(1)}, f32[1024,128]{1,0:T(8,128)}, u32[]{:S(2)}) copy-start(f32[1024,128]{1,0:T(8,128)} %get-tuple-element.17) | copy-start | bytes 1572868
where the time goes:
time: 85.6 us; the launch traced here: 84.1 us
  Pallas kernels  80.1 us (94%)
  local copies, waits for them, and re-layouts  2.72 us (3%)
  between operations  1.31 us (2%)
    pallas_call x2, Pallas kernels, body(): pl.pallas_call(functools.partial(update_kernel, n, final, modes), name='u...  59.1 us
    pallas_call x2, Pallas kernels, body(): gradient(offsets.T, counts, padded, probe_now, measured, tables[0], table...  15.1 us
    pallas_call x1, Pallas kernels, body(): pl.pallas_call(functools.partial(halo_kernel, n), name='halo', out_shape=...  5.92 us
    unnamed x4, local copies, waits for them, and re-layouts  2.72 us

commit v1 on v0

v1 whole, which is shorter than its diff:
```python
import functools
import math

import jax
import jax.numpy as jnp
import numpy as np
from jax import lax
from jax.experimental import pallas as pl
from jax.experimental.pallas import tpu as pltpu
from jax.sharding import PartitionSpec as P

ITERS = 2
object_rate = 0.2
probe_rate = 0.5
SUBLANES = 8
VMEM = pl.BlockSpec(memory_space=pltpu.VMEM)
ANY = pl.BlockSpec(memory_space=pl.ANY)
SMEM = pl.BlockSpec(memory_space=pltpu.SMEM)
MESH = pl.DeviceIdType.MESH


def dft_tables(length):
    index = np.arange(length)
    phase = 2.0 * math.pi / length * (index[:, None] * index[None, :] % length)
    cosine = np.cos(phase) / math.sqrt(length)
    sine = -np.sin(phase) / math.sqrt(length)
    forward = np.block([[cosine, -sine], [sine, cosine]]).astype(np.float32)
    backward = np.block([[cosine, sine], [-sine, cosine]]).astype(np.float32)
    tables = []
    for table in (forward, backward):
        high = table.astype(jnp.bfloat16)
        tables.append(high)
        tables.append((table - high.astype(np.float32)).astype(jnp.bfloat16))
    return jnp.asarray(np.stack(tables))


def halves(x):
    high = x.astype(jnp.bfloat16)
    return high, (x - high.astype(jnp.float32)).astype(jnp.bfloat16)


def greet(me, n, devices):
    barrier = pltpu.get_barrier_semaphore()

    def signal(device):
        pl.semaphore_signal(barrier, inc=1, device_id={"row": device}, device_id_type=MESH)

    pl.when(me > 0)(lambda: signal(me - 1))
    pl.when(me < n - 1)(lambda: signal(me + 1))
    for device in devices:
        signal(device)
    inside = (me > 0) & (me < n - 1)
    pl.when(inside)(lambda: pl.semaphore_wait(barrier, len(devices) + 2))
    pl.when(jnp.logical_not(inside))(lambda: pl.semaphore_wait(barrier, len(devices) + 1))


def remote(src, dst, send, recv, device):
    return pltpu.make_async_remote_copy(
        src_ref=src, dst_ref=dst, send_sem=send, recv_sem=recv,
        device_id={"row": device}, device_id_type=MESH,
    )


def exchange(me, n, array, to_up, to_down, from_up, from_down, sems):
    up = remote(to_up, from_down, sems.at[0], sems.at[1], me - 1)
    down = remote(to_down, from_up, sems.at[2], sems.at[3], me + 1)

    def start():
        pl.when(me > 0)(up.start)
        pl.when(me < n - 1)(down.start)

    def wait():
        @pl.when(me > 0)
        def _():
            up.wait_send()
            down.wait_recv()

        @pl.when(me < n - 1)
        def _():
            down.wait_send()
            up.wait_recv()

    return start, wait


def steps_kernel(
    n, groups, offsets, counts, tile, probe_in, measured_in, tables_in, obj_out, probe_out,
    obj, grad, wide, windows, far, x2, y2, target, resid, slot_grad, probes, probe_grad,
    total, from_mate, from_chip, energies, energy_chip, edge_up, edge_down, last_up, last_down,
    tables, load_sems, halo_sems, edge_sems, energy_sems, energy_out, energy_in,
    mate_sems, sum_out, sum_in, new_out, new_in,
):
    me = lax.axis_index("row")
    slots, length = target.shape[0], target.shape[1]
    blocks = obj.shape[1]
    padded_rows = obj.shape[2]
    cols = blocks * length
    margin = length // 2
    rows = padded_rows - 2 * margin
    pad = padded_rows - length
    half = probe_grad.shape[1]
    modes = half // length
    per_group = modes // groups
    group_rows = half // groups
    chips = n // 2
    shard = group_rows // chips
    core, chip = me % 2, me // 2
    mate = me + 1 - 2 * core
    f32 = jnp.float32
    both = 2 * length

    def peer(d):
        return lax.rem(chip + d, chips)

    def device(q):
        return 2 * q + core

    loads = [
        pltpu.make_async_copy(src, dst, load_sems.at[i])
        for i, (src, dst) in enumerate(
            [
                (tile.at[:, :, j * length : (j + 1) * length], obj.at[:, j, margin : margin + rows])
                for j in range(blocks)
            ]
            + [(probe_in, probes.at[0]), (tables_in, tables), (measured_in, target)]
        )
    ]
    for load in loads:
        load.start()
    greet(me, n, [mate] + [device(peer(d)) for d in range(1, chips)])
    for load in loads[:blocks]:
        load.wait()
    start_halo, wait_halo = exchange(
        me, n, obj,
        obj.at[:, :, margin : 2 * margin], obj.at[:, :, rows : rows + margin],
        obj.at[:, :, :margin], obj.at[:, :, margin + rows :], halo_sems,
    )
    start_halo()
    edge_zero = jnp.zeros((2, blocks, margin, length), f32)

    def clear_outside():
        @pl.when(me == 0)
        def _():
            obj[:, :, :margin] = edge_zero

        @pl.when(me == n - 1)
        def _():
            obj[:, :, margin + rows :] = edge_zero

    clear_outside()

    @pl.when(me == 0)
    def _():
        edge_up[...] = jnp.zeros_like(edge_up)
        last_up[...] = jnp.zeros_like(last_up)

    @pl.when(me == n - 1)
    def _():
        edge_down[...] = jnp.zeros_like(edge_down)
        last_down[...] = jnp.zeros_like(last_down)

    wide[...] = jnp.zeros_like(wide)
    for load in loads[blocks:]:
        load.wait()
    wait_halo()

    def live(s):
        return jnp.where(counts[0] > s, 1.0, 0.0).astype(f32)

    def table(i, axis):
        high, low = tables[2 * i], tables[2 * i + 1]
        return jnp.concatenate([high, high, low], axis=axis)

    def put_x(s, part, value):
        high, low = halves(value)
        c = slice(s * length, (s + 1) * length)
        x2[part * length : (part + 1) * length, c] = high
        x2[both + part * length : both + (part + 1) * length, c] = low

    def put_y(s, part, value):
        high, low = halves(value)
        r = slice(s * length, (s + 1) * length)
        y2[r, part * length : (part + 1) * length] = high
        y2[r, both + part * length : both + (part + 1) * length] = low

    def left_dot(i):
        x = jnp.concatenate([x2[...], x2[:both]], axis=0)
        return jnp.dot(table(i, 1), x, preferred_element_type=f32)

    def right_dot(i):
        y = jnp.concatenate([y2[...], y2[:, :both]], axis=1)
        return jnp.dot(y, table(i, 0), preferred_element_type=f32)

    def cell(s, part):
        return slice(s * length, (s + 1) * length), slice(part * length, (part + 1) * length)

    def mode_rows(k):
        return pl.ds(pl.multiple_of(k * length, length), length)

    def group_region(g):
        return pl.ds(pl.multiple_of(g * group_rows, group_rows), group_rows)

    def shard_region(g, q):
        return pl.ds(pl.multiple_of(g * group_rows + q * shard, shard), shard)

    def energy_to_mate():
        return remote(energies.at[0], energies.at[1], energy_sems.at[0], energy_sems.at[1], mate)

    def energy_to(q, d):
        return remote(
            energies.at[2], energy_chip.at[chip], energy_out.at[d], energy_in.at[chip], device(q)
        )

    def energy_from(q):
        return remote(
            energies.at[2], energy_chip.at[q], energy_out.at[0], energy_in.at[q], device(q)
        )

    def grad_to_mate(g):
        return remote(
            probe_grad.at[1 - core, group_region(g)], from_mate.at[group_region(g)],
            mate_sems.at[0, g], mate_sems.at[1, g], mate,
        )

    def sum_to(g, q, d):
        return remote(
            total.at[shard_region(g, q)], from_chip.at[g, chip],
            sum_out.at[g, d], sum_in.at[g, chip], device(q),
        )

    def sum_from(g, q):
        return remote(
            total.at[shard_region(g, q)], from_chip.at[g, q],
            sum_out.at[g, 0], sum_in.at[g, q], device(q),
        )

    for sweep in range(ITERS):
        final = sweep == ITERS - 1
        probe = probes.at[sweep]
        fresh = probes.at[sweep + 1]

        def cut(s, carry):
            row = offsets[0, s] + margin
            shift = lax.rem(cols - offsets[1, s], cols)
            power = jnp.zeros((length, length), f32)
            for c in range(2):
                whole = jnp.concatenate(
                    [obj[c, j, pl.ds(row, length), :] for j in range(blocks)], axis=1
                )
                value = pltpu.roll(whole, shift, 1)[:, :length]
                windows[s, c] = value
                power = power + value * value
            return carry + live(s) * power.reshape(-1, SUBLANES, length).sum(axis=0)

        energies[0] = lax.fori_loop(0, slots, cut, jnp.zeros((SUBLANES, length), f32))
        energy_to_mate().start()
        resid[...] = jnp.zeros_like(resid)

        def forward(k):
            pr = probe[mode_rows(k), :]
            pi = probe[pl.ds(pl.multiple_of(half + k * length, length), length), :]
            for s in range(slots):
                wr, wi = windows[s, 0], windows[s, 1]
                put_x(s, 0, pr * wr - pi * wi)
                put_x(s, 1, pr * wi + pi * wr)
            left = left_dot(0)
            for s in range(slots):
                for part in range(2):
                    b, a = cell(s, part)
                    put_y(s, part, left[a, b])
            value = right_dot(1)
            far[k] = value
            for s in range(slots):
                (r, re), (_, im) = cell(s, 0), cell(s, 1)
                resid[s] += value[r, re] * value[r, re] + value[r, im] * value[r, im]

        def new_to(g, q, d, fresh=fresh):
            part = fresh.at[pl.ds(pl.multiple_of(core * half + g * group_rows + chip * shard, shard), shard)]
            return remote(part, part, new_out.at[g, d], new_in.at[g, chip], device(q))

        def new_from(g, q, fresh=fresh):
            part = fresh.at[pl.ds(pl.multiple_of(core * half + g * group_rows + q * shard, shard), shard)]
            return remote(part, part, new_out.at[g, 0], new_in.at[g, q], device(q))

        def new_to_mate(g, side, fresh=fresh):
            part = fresh.at[pl.ds(pl.multiple_of(side * half + g * group_rows, group_rows), group_rows)]
            return remote(part, part, mate_sems.at[2, g], mate_sems.at[3, g], mate)

        def forward_group(g, carry):
            if sweep:
                part = probe.at[pl.ds(pl.multiple_of((1 - core) * half + g * group_rows, group_rows), group_rows)]
                remote(part, part, mate_sems.at[2, g], mate_sems.at[3, g], mate).wait_recv()
            for m in range(per_group):
                forward(g * per_group + m)
            return carry

        lax.fori_loop(0, groups, forward_group, 0)

        if sweep:
            def settle(g, carry):
                part = probe.at[pl.ds(pl.multiple_of(core * half + g * group_rows, group_rows), group_rows)]
                remote(part, part, mate_sems.at[2, g], mate_sems.at[3, g], mate).wait_send()
                return carry

            lax.fori_loop(0, groups, settle, 0)

        energy_to_mate().wait_recv()
        energies[2] = energies[0] + energies[1]
        for d in range(1, chips):
            energy_to(peer(d), d).start()
        for s in range(slots):
            resid[s] = (resid[s] - target[s]) * live(s)
        slot_grad[...] = jnp.zeros_like(slot_grad)

        def backward(k):
            for s in range(slots):
                for part in range(2):
                    r, c = cell(s, part)
                    put_y(s, part, resid[s] * far[k, r, c])
            right = right_dot(0)
            for s in range(slots):
                for part in range(2):
                    r, c = cell(s, part)
                    put_x(s, part, right[r, c])
            back = left_dot(1)
            pr = probe[mode_rows(k), :]
            pi = probe[pl.ds(pl.multiple_of(half + k * length, length), length), :]
            sr = jnp.zeros((length, length), f32)
            si = jnp.zeros((length, length), f32)
            for s in range(slots):
                (b, re), (_, im) = cell(s, 0), cell(s, 1)
                br, bi = back[re, b], back[im, b]
                wr, wi = windows[s, 0], windows[s, 1]
                slot_grad[s, 0] += pr * br + pi * bi
                slot_grad[s, 1] += pr * bi - pi * br
                sr = sr + (wr * br + wi * bi)
                si = si + (wr * bi - wi * br)
            probe_grad[0, mode_rows(k), :] = sr
            probe_grad[1, mode_rows(k), :] = si

        def pass_sums(g):
            grad_to_mate(g).wait_recv()
            region = group_region(g)
            total[region] = probe_grad[core, region] + from_mate[region]
            for d in range(1, chips):
                sum_to(g, peer(d), d).start()

        def backward_group(g, carry):
            for m in range(per_group):
                backward(g * per_group + m)
            grad_to_mate(g).start()
            pl.when(g > 0)(lambda: pass_sums(g - 1))
            return carry

        lax.fori_loop(0, groups, backward_group, 0)

        zeros = jnp.zeros((length, cols - length), f32)
        for s in range(slots):
            for c in range(2):
                placed = pltpu.roll(
                    jnp.concatenate([slot_grad[s, c], zeros], axis=1), offsets[1, s], 1
                )
                for j in range(blocks):
                    value = placed[:, j * length : (j + 1) * length]
                    if s == 0:
                        grad[c, j, :length] = value
                    elif s == 1:
                        grad[c, j, pad:] = value
                    else:
                        wide[s - 2, c, j, pad : pad + length] = value
        grad[:, :, length:pad] = jnp.zeros((2, blocks, pad - length, length), f32)
        pass_sums(groups - 1)
        for s in range(2, slots):
            start = pad - margin - offsets[0, s]
            for c in range(2):
                for j in range(blocks):
                    grad[c, j] += wide[s - 2, c, j, pl.ds(start, padded_rows), :]

        edge = margin if final else 2 * margin
        up, down = (last_up, last_down) if final else (edge_up, edge_down)
        start_edge, wait_edge = exchange(
            me, n, grad, grad.at[:, :, :edge], grad.at[:, :, padded_rows - edge :],
            up, down, edge_sems.at[sweep],
        )
        start_edge()

        power = jnp.zeros((length, length), f32)
        for k in range(2 * modes):
            p = probe[k * length : (k + 1) * length, :]
            power = power + p * p
        step = object_rate / jnp.max(power, axis=(0, 1), keepdims=True)
        base = margin if final else 0
        inner = slice(base + edge, padded_rows - base - edge)
        obj[:, :, inner] = obj[:, :, inner] - step * grad[:, :, inner]

        energy = energies[2]
        for d in range(1, chips):
            energy_from(peer(d)).wait_recv()
            energy = energy + energy_chip[peer(d)]
        probe_step = probe_rate * length * length / jnp.sum(energy, axis=(0, 1), keepdims=True)

        def renew(g, carry):
            share = total[shard_region(g, chip)]
            for d in range(1, chips):
                sum_from(g, peer(d)).wait_recv()
                share = share + from_chip[g, peer(d)]
            own = pl.ds(pl.multiple_of(core * half + g * group_rows + chip * shard, shard), shard)
            fresh[own] = probe[own] - probe_step * share
            for d in range(1, chips):
                new_to(g, peer(d), d).start()
            return carry

        lax.fori_loop(0, groups, renew, 0)
        wait_edge()
        top = slice(base, base + edge)
        low = slice(padded_rows - base - edge, padded_rows - base)
        obj[:, :, top] = obj[:, :, top] - step * (grad[:, :, top] + up[...])
        obj[:, :, low] = obj[:, :, low] - step * (grad[:, :, low] + down[...])
        if final:
            stores = [
                pltpu.make_async_copy(
                    obj.at[:, j, margin : margin + rows],
                    obj_out.at[:, :, j * length : (j + 1) * length], load_sems.at[j],
                )
                for j in range(blocks)
            ]
            for store in stores:
                store.start()
        else:
            clear_outside()

        def share_new(g, carry):
            for d in range(1, chips):
                new_from(g, peer(d)).wait_recv()
            new_to_mate(g, core).start()
            return carry

        lax.fori_loop(0, groups, share_new, 0)

        def finish(g, carry):
            grad_to_mate(g).wait_send()
            for d in range(1, chips):
                sum_to(g, peer(d), d).wait_send()
                new_to(g, peer(d), d).wait_send()
            return carry

        energy_to_mate().wait_send()
        for d in range(1, chips):
            energy_to(peer(d), d).wait_send()
        lax.fori_loop(0, groups, finish, 0)
        if final:
            def arrive(g, carry):
                new_to_mate(g, 1 - core).wait_recv()
                new_to_mate(g, core).wait_send()
                return carry

            lax.fori_loop(0, groups, arrive, 0)
            result = pltpu.make_async_copy(fresh, probe_out, load_sems.at[blocks])
            result.start()
            for store in stores:
                store.wait()
            result.wait()


def body(object_tile, probe_modes, measured, offsets, counts):
    n = lax.axis_size("row")
    parts, rows, cols = object_tile.shape
    modes, length = probe_modes.shape[1], probe_modes.shape[2]
    slots = measured.shape[0]
    margin = length // 2
    blocks = cols // length
    padded = rows + 2 * margin
    half = modes * length
    chips = n // 2
    groups = modes
    while groups > 1 and (modes % groups or half // groups % (chips * SUBLANES)):
        groups -= 1
    shard = half // groups // chips
    f32, bf16 = jnp.float32, jnp.bfloat16
    dma = pltpu.SemaphoreType.DMA
    tables = dft_tables(length)

    def vmem(*shape, dtype=f32):
        return pltpu.VMEM(shape, dtype)

    new_object, fresh = pl.pallas_call(
        functools.partial(steps_kernel, n, groups),
        name="steps",
        out_shape=[
            jax.ShapeDtypeStruct(object_tile.shape, f32),
            jax.ShapeDtypeStruct((2 * half, length), f32),
        ],
        in_specs=[SMEM, SMEM] + [ANY] * 4,
        out_specs=[ANY] * 2,
        scratch_shapes=[
            vmem(2, blocks, padded, length),
            vmem(2, blocks, padded, length),
            vmem(max(slots - 2, 1), 2, blocks, 2 * padded - length, length),
            vmem(slots, 2, length, length),
            vmem(modes, slots * length, 2 * length),
            vmem(4 * length, slots * length, dtype=bf16),
            vmem(slots * length, 4 * length, dtype=bf16),
            vmem(slots, length, length),
            vmem(slots, length, length),
            vmem(slots, 2, length, length),
            vmem(ITERS + 1, 2 * half, length),
            vmem(2, half, length),
            vmem(half, length),
            vmem(half, length),
            vmem(groups, chips, shard, length),
            vmem(3, SUBLANES, length),
            vmem(chips, SUBLANES, length),
            vmem(2, blocks, 2 * margin, length),
            vmem(2, blocks, 2 * margin, length),
            vmem(2, blocks, margin, length),
            vmem(2, blocks, margin, length),
            vmem(*tables.shape, dtype=bf16),
            dma((blocks + 3,)), dma((4,)), dma((ITERS, 4)),
            dma((2,)), dma((chips,)), dma((chips,)),
            dma((4, groups)),
            dma((groups, chips)), dma((groups, chips)), dma((groups, chips)), dma((groups, chips)),
        ],
        compiler_params=pltpu.CompilerParams(collective_id=0, has_side_effects=True),
    )(
        offsets.T, counts, object_tile, probe_modes.reshape(2 * half, length), measured, tables
    )
    return (new_object, fresh.reshape(probe_modes.shape))


def solution(mesh):
    return jax.shard_map(
        body,
        mesh=mesh,
        in_specs=(
            P(None, ("parts", "row"), None),
            P(),
            P(("parts", "row"), None, None),
            P(("parts", "row"), None),
            P(("parts", "row")),
        ),
        out_specs=(P(None, ("parts", "row"), None), P("parts", None, None, None)),
        check_vma=False,
    )
```

time: 85.6 us -> 62.3 us (0.73); the launches traced: 84.1 us -> 62.1 us
  Pallas kernels: 80.1 us -> 58.1 us
    pallas_call x5 -> x1, Pallas kernels: 80.1 us -> 58.1 us  [body(): pl.pallas_call(functools.partial(steps_kernel, n, groups), name='steps',...]
where the time goes in v1:
time: 62.3 us; the launch traced here: 62.1 us
  Pallas kernels  58.1 us (93%)
  local copies, waits for them, and re-layouts  2.72 us (4%)
  between operations  1.29 us (2%)
    pallas_call x1, Pallas kernels, body(): pl.pallas_call(functools.partial(steps_kernel, n, groups), name='steps',...  58.1 us
    unnamed x4, local copies, waits for them, and re-layouts  2.72 us

profile of v1, /device:TPU:0, one launch (start us, length us, event | category | flops | bytes accessed | tf_op | source)
XLA Modules:
  0.0 62.1 jit_solution(3396851210383567282)
XLA Ops:
  1.3 58.1 %steps.1 = (f32[2,256,256]{2,1,0:T(8,128)}, f32[1024,128]{1,0:T(8,128)}) custom-call(s32[2,4]{1,0:T(2,128)} %bitcast.5, s32[1]{0:T(128)S(6)} %copy.10.counts, f32[2,256,256]{2,1,0:T(8,128)} %tile.1, f32[1024,128]{1,0:T(8,128)} %bitcast.4, f32[4,128,128]{2,1,0:T(8,128)} %measured_in.1, bf16[4,256,256]{2,1,0:T(8,128)(2,1)} %constant.2.clone.tables_in), custom_call_target="tpu_custom_call" | custom-call | tf_op jit(solution)/shard_map/steps/pallas_call | solution.py:486
  59.4 0.0 copy-start
  59.4 1.9 %copy.11 = f32[2,256,256]{2,1,0:T(8,128)} copy(f32[2,256,256]{2,1,0:T(8,128)} %get-tuple-element.8) | data formatting | bytes 1048576
  61.3 0.0 copy-done
  61.3 0.8 %copy.12 = f32[2,4,128,128]{3,2,1,0:T(8,128)} copy(f32[2,4,128,128]{3,2,1,0:T(8,128)S(1)} %bitcast.3) | data formatting | bytes 1048576
Async XLA Ops:
  59.4 1.9 %copy-start = (f32[1024,128]{1,0:T(8,128)S(1)}, f32[1024,128]{1,0:T(8,128)}, u32[]{:S(2)}) copy-start(f32[1024,128]{1,0:T(8,128)} %get-tuple-element.5) | copy-start | bytes 1572868

commit v2 on v1

--- a/solution.py
+++ b/solution.py
@@ -39,19 +39,21 @@
     return high, (x - high.astype(jnp.float32)).astype(jnp.bfloat16)
 
 
-def greet(me, n, devices):
+def both_sides(me, n, distance, up, down):
+    pl.when(me >= distance)(lambda: up(me - distance))
+    pl.when(me + distance < n)(lambda: down(me + distance))
+
+
+def greet(me, n):
     barrier = pltpu.get_barrier_semaphore()
 
     def signal(device):
         pl.semaphore_signal(barrier, inc=1, device_id={"row": device}, device_id_type=MESH)
 
-    pl.when(me > 0)(lambda: signal(me - 1))
-    pl.when(me < n - 1)(lambda: signal(me + 1))
-    for device in devices:
-        signal(device)
+    both_sides(me, n, 1, signal, signal)
     inside = (me > 0) & (me < n - 1)
-    pl.when(inside)(lambda: pl.semaphore_wait(barrier, len(devices) + 2))
-    pl.when(jnp.logical_not(inside))(lambda: pl.semaphore_wait(barrier, len(devices) + 1))
+    pl.when(inside)(lambda: pl.semaphore_wait(barrier, 2))
+    pl.when(jnp.logical_not(inside))(lambda: pl.semaphore_wait(barrier, 1))
 
 
 def remote(src, dst, send, recv, device):
@@ -84,11 +86,11 @@
 
 
 def steps_kernel(
-    n, groups, offsets, counts, tile, probe_in, measured_in, tables_in, obj_out, probe_out,
-    obj, grad, wide, windows, far, x2, y2, target, resid, slot_grad, probes, probe_grad,
+    n, groups, teams, offsets, counts, tile, probe_in, measured_in, tables_in, obj, last_probes,
+    grad, wide, windows, far, target, resid, slot_grad, probes, probe_grad,
     total, from_mate, from_chip, energies, energy_chip, edge_up, edge_down, last_up, last_down,
     tables, load_sems, halo_sems, edge_sems, energy_sems, energy_out, energy_in,
-    mate_sems, sum_out, sum_in, new_out, new_in,
+    mate_sems, heard, sum_out, sum_in, new_out, new_in,
 ):
     me = lax.axis_index("row")
     slots, length = target.shape[0], target.shape[1]
@@ -127,7 +129,28 @@
     ]
     for load in loads:
         load.start()
-    greet(me, n, [mate] + [device(peer(d)) for d in range(1, chips)])
+    greet(me, n)
+    spans = []
+    while 2 ** len(spans) < n - 1:
+        spans.append(2 ** len(spans))
+
+    def tell(i):
+        def signal(side):
+            return lambda device: pl.semaphore_signal(
+                heard.at[i, side], inc=1, device_id={"row": device}, device_id_type=MESH
+            )
+
+        if i < len(spans):
+            both_sides(me, n, spans[i], signal(1), signal(0))
+
+    def hear(i):
+        def wait(side):
+            return lambda device: pl.semaphore_wait(heard.at[i, side], 1)
+
+        if i < len(spans):
+            both_sides(me, n, spans[i], wait(0), wait(1))
+            tell(i + 1)
+
     for load in loads[:blocks]:
         load.wait()
     start_halo, wait_halo = exchange(
@@ -136,6 +159,7 @@
         obj.at[:, :, :margin], obj.at[:, :, margin + rows :], halo_sems,
     )
     start_halo()
+    tell(0)
     edge_zero = jnp.zeros((2, blocks, margin, length), f32)
 
     def clear_outside():
@@ -163,6 +187,7 @@
     for load in loads[blocks:]:
         load.wait()
     wait_halo()
+    hear(0)
 
     def live(s):
         return jnp.where(counts[0] > s, 1.0, 0.0).astype(f32)
@@ -171,25 +196,17 @@
         high, low = tables[2 * i], tables[2 * i + 1]
         return jnp.concatenate([high, high, low], axis=axis)
 
-    def put_x(s, part, value):
-        high, low = halves(value)
-        c = slice(s * length, (s + 1) * length)
-        x2[part * length : (part + 1) * length, c] = high
-        x2[both + part * length : both + (part + 1) * length, c] = low
-
-    def put_y(s, part, value):
-        high, low = halves(value)
-        r = slice(s * length, (s + 1) * length)
-        y2[r, part * length : (part + 1) * length] = high
-        y2[r, both + part * length : both + (part + 1) * length] = low
-
-    def left_dot(i):
-        x = jnp.concatenate([x2[...], x2[:both]], axis=0)
-        return jnp.dot(table(i, 1), x, preferred_element_type=f32)
-
-    def right_dot(i):
-        y = jnp.concatenate([y2[...], y2[:, :both]], axis=1)
-        return jnp.dot(y, table(i, 0), preferred_element_type=f32)
+    def left_dot(i, real, imag):
+        x = jnp.concatenate([jnp.concatenate(real, axis=1), jnp.concatenate(imag, axis=1)], axis=0)
+        high, low = halves(x)
+        return jnp.dot(table(i, 1), jnp.concatenate([high, low, high], axis=0), preferred_element_type=f32)
+
+    def right_dot(i, real, imag):
+        y = jnp.concatenate([jnp.concatenate(real, axis=0), jnp.concatenate(imag, axis=0)], axis=1)
+        high, low = halves(y)
+        return jnp.dot(jnp.concatenate([high, low, high], axis=1), table(i, 0), preferred_element_type=f32)
+
+    team = slots // teams
 
     def cell(s, part):
         return slice(s * length, (s + 1) * length), slice(part * length, (part + 1) * length)
@@ -234,10 +251,40 @@
             sum_out.at[g, 0], sum_in.at[g, q], device(q),
         )
 
+    def rows_of(side, g, first, count):
+        return pl.ds(pl.multiple_of(side * half + g * group_rows + first, count), count)
+
+    def new_to(fresh, g, q, d):
+        part = fresh.at[rows_of(core, g, chip * shard, shard)]
+        return remote(part, part, new_out.at[g, d], new_in.at[g, chip], device(q))
+
+    def new_from(fresh, g, q):
+        part = fresh.at[rows_of(core, g, q * shard, shard)]
+        return remote(part, part, new_out.at[g, 0], new_in.at[g, q], device(q))
+
+    def new_to_mate(fresh, g, side):
+        part = fresh.at[rows_of(side, g, 0, group_rows)]
+        return remote(part, part, mate_sems.at[2, g], mate_sems.at[3, g], mate)
+
+    def share_new(fresh, g):
+        for d in range(1, chips):
+            new_from(fresh, g, peer(d)).wait_recv()
+        new_to_mate(fresh, g, core).start()
+
+    def finish(fresh, g):
+        grad_to_mate(g).wait_send()
+        for d in range(1, chips):
+            sum_to(g, peer(d), d).wait_send()
+            new_to(fresh, g, peer(d), d).wait_send()
+        new_to_mate(fresh, g, core).wait_send()
+
+    def loop(count, step):
+        lax.fori_loop(0, count, lambda i, carry: (step(i), carry)[1], 0)
+
     for sweep in range(ITERS):
         final = sweep == ITERS - 1
         probe = probes.at[sweep]
-        fresh = probes.at[sweep + 1]
+        fresh = last_probes if final else probes.at[sweep + 1]
 
         def cut(s, carry):
             row = offsets[0, s] + margin
@@ -252,6 +299,10 @@
                 power = power + value * value
             return carry + live(s) * power.reshape(-1, SUBLANES, length).sum(axis=0)
 
+        if sweep:
+            energy_to_mate().wait_send()
+            for d in range(1, chips):
+                energy_to(peer(d), d).wait_send()
         energies[0] = lax.fori_loop(0, slots, cut, jnp.zeros((SUBLANES, length), f32))
         energy_to_mate().start()
         resid[...] = jnp.zeros_like(resid)
@@ -259,84 +310,84 @@
         def forward(k):
             pr = probe[mode_rows(k), :]
             pi = probe[pl.ds(pl.multiple_of(half + k * length, length), length), :]
-            for s in range(slots):
-                wr, wi = windows[s, 0], windows[s, 1]
-                put_x(s, 0, pr * wr - pi * wi)
-                put_x(s, 1, pr * wi + pi * wr)
-            left = left_dot(0)
-            for s in range(slots):
-                for part in range(2):
-                    b, a = cell(s, part)
-                    put_y(s, part, left[a, b])
-            value = right_dot(1)
-            far[k] = value
-            for s in range(slots):
-                (r, re), (_, im) = cell(s, 0), cell(s, 1)
-                resid[s] += value[r, re] * value[r, re] + value[r, im] * value[r, im]
-
-        def new_to(g, q, d, fresh=fresh):
-            part = fresh.at[pl.ds(pl.multiple_of(core * half + g * group_rows + chip * shard, shard), shard)]
-            return remote(part, part, new_out.at[g, d], new_in.at[g, chip], device(q))
-
-        def new_from(g, q, fresh=fresh):
-            part = fresh.at[pl.ds(pl.multiple_of(core * half + g * group_rows + q * shard, shard), shard)]
-            return remote(part, part, new_out.at[g, 0], new_in.at[g, q], device(q))
-
-        def new_to_mate(g, side, fresh=fresh):
-            part = fresh.at[pl.ds(pl.multiple_of(side * half + g * group_rows, group_rows), group_rows)]
-            return remote(part, part, mate_sems.at[2, g], mate_sems.at[3, g], mate)
-
-        def forward_group(g, carry):
+            def enter(h):
+                real, imag = [], []
+                for s in range(h * team, (h + 1) * team):
+                    wr, wi = windows[s, 0], windows[s, 1]
+                    real.append(pr * wr - pi * wi)
+                    imag.append(pr * wi + pi * wr)
+                return left_dot(0, real, imag)
+
+            def leave(h, left):
+                real = [left[:length, s * length : (s + 1) * length] for s in range(team)]
+                imag = [left[length:, s * length : (s + 1) * length] for s in range(team)]
+                value = right_dot(1, real, imag)
+                far[k, h * team * length : (h + 1) * team * length] = value
+                for s in range(team):
+                    (r, re), (_, im) = cell(s, 0), cell(s, 1)
+                    resid[h * team + s] += value[r, re] * value[r, re] + value[r, im] * value[r, im]
+
+            left = [enter(h) for h in range(teams)]
+            for h in range(teams):
+                leave(h, left[h])
+
+        def forward_group(g):
             if sweep:
-                part = probe.at[pl.ds(pl.multiple_of((1 - core) * half + g * group_rows, group_rows), group_rows)]
-                remote(part, part, mate_sems.at[2, g], mate_sems.at[3, g], mate).wait_recv()
+                pl.when(g + 1 < groups)(lambda: share_new(probe, jnp.minimum(g + 1, groups - 1)))
+                new_to_mate(probe, g, 1 - core).wait_recv()
             for m in range(per_group):
                 forward(g * per_group + m)
-            return carry
-
-        lax.fori_loop(0, groups, forward_group, 0)
 
         if sweep:
-            def settle(g, carry):
-                part = probe.at[pl.ds(pl.multiple_of(core * half + g * group_rows, group_rows), group_rows)]
-                remote(part, part, mate_sems.at[2, g], mate_sems.at[3, g], mate).wait_send()
-                return carry
-
-            lax.fori_loop(0, groups, settle, 0)
+            share_new(probe, 0)
+        loop(groups, forward_group)
+        if sweep:
+            loop(groups, lambda g: finish(probe, g))
 
         energy_to_mate().wait_recv()
         energies[2] = energies[0] + energies[1]
-        for d in range(1, chips):
-            energy_to(peer(d), d).start()
+        if not sweep:
+            hear(1)
         for s in range(slots):
             resid[s] = (resid[s] - target[s]) * live(s)
         slot_grad[...] = jnp.zeros_like(slot_grad)
 
-        def backward(k):
-            for s in range(slots):
-                for part in range(2):
-                    r, c = cell(s, part)
-                    put_y(s, part, resid[s] * far[k, r, c])
-            right = right_dot(0)
-            for s in range(slots):
-                for part in range(2):
-                    r, c = cell(s, part)
-                    put_x(s, part, right[r, c])
-            back = left_dot(1)
+        def backward(k, between):
+            def enter(h):
+                parts = [
+                    [resid[s] * far[k, slice(s * length, (s + 1) * length), c] for s in range(h * team, (h + 1) * team)]
+                    for c in (slice(0, length), slice(length, both))
+                ]
+                return right_dot(0, *parts)
+
+            def leave(right):
+                real = [right[s * length : (s + 1) * length, :length] for s in range(team)]
+                imag = [right[s * length : (s + 1) * length, length:] for s in range(team)]
+                return left_dot(1, real, imag)
+
+            right = [enter(h) for h in range(teams)]
+            back = [leave(value) for value in right]
+
+            def value_of(s):
+                (b, re), (_, im) = cell(s % team, 0), cell(s % team, 1)
+                return back[s // team][re, b], back[s // team][im, b]
+
             pr = probe[mode_rows(k), :]
             pi = probe[pl.ds(pl.multiple_of(half + k * length, length), length), :]
             sr = jnp.zeros((length, length), f32)
             si = jnp.zeros((length, length), f32)
             for s in range(slots):
-                (b, re), (_, im) = cell(s, 0), cell(s, 1)
-                br, bi = back[re, b], back[im, b]
+                br, bi = value_of(s)
                 wr, wi = windows[s, 0], windows[s, 1]
-                slot_grad[s, 0] += pr * br + pi * bi
-                slot_grad[s, 1] += pr * bi - pi * br
                 sr = sr + (wr * br + wi * bi)
                 si = si + (wr * bi - wi * br)
             probe_grad[0, mode_rows(k), :] = sr
             probe_grad[1, mode_rows(k), :] = si
+            between()
+            for s in range(slots):
+                br, bi = value_of(s)
+                slot_grad[s, 0] += pr * br + pi * bi
+                slot_grad[s, 1] += pr * bi - pi * br
 
         def pass_sums(g):
             grad_to_mate(g).wait_recv()
@@ -345,14 +396,28 @@
             for d in range(1, chips):
                 sum_to(g, peer(d), d).start()
 
-        def backward_group(g, carry):
+        def hear_rest():
+            if not sweep:
+                for i in range(3 if groups > 1 else 2, len(spans)):
+                    hear(i)
+            for d in range(1, chips):
+                energy_to(peer(d), d).start()
+
+        def backward_group(g):
+            def send():
+                grad_to_mate(g).start()
+                if groups > 1:
+                    if not sweep:
+                        pl.when(g == 0)(lambda: hear(2))
+                    pl.when(g == 1)(hear_rest)
+                pl.when(g > 0)(lambda: pass_sums(jnp.maximum(g - 1, 0)))
+
             for m in range(per_group):
-                backward(g * per_group + m)
-            grad_to_mate(g).start()
-            pl.when(g > 0)(lambda: pass_sums(g - 1))
-            return carry
-
-        lax.fori_loop(0, groups, backward_group, 0)
+                backward(g * per_group + m, send if m == per_group - 1 else lambda: None)
+
+        loop(groups, backward_group)
+        if groups == 1:
+            hear_rest()
 
         zeros = jnp.zeros((length, cols - length), f32)
         for s in range(slots):
@@ -382,7 +447,8 @@
             me, n, grad, grad.at[:, :, :edge], grad.at[:, :, padded_rows - edge :],
             up, down, edge_sems.at[sweep],
         )
-        start_edge()
+        if not final:
+            start_edge()
 
         power = jnp.zeros((length, length), f32)
         for k in range(2 * modes):
@@ -399,67 +465,49 @@
             energy = energy + energy_chip[peer(d)]
         probe_step = probe_rate * length * length / jnp.sum(energy, axis=(0, 1), keepdims=True)
 
-        def renew(g, carry):
+        def renew(g):
             share = total[shard_region(g, chip)]
             for d in range(1, chips):
                 sum_from(g, peer(d)).wait_recv()
                 share = share + from_chip[g, peer(d)]
-            own = pl.ds(pl.multiple_of(core * half + g * group_rows + chip * shard, shard), shard)
+            own = rows_of(core, g, chip * shard, shard)
             fresh[own] = probe[own] - probe_step * share
             for d in range(1, chips):
-                new_to(g, peer(d), d).start()
-            return carry
-
-        lax.fori_loop(0, groups, renew, 0)
+                new_to(fresh, g, peer(d), d).start()
+
+        loop(groups, renew)
+        if final:
+            start_edge()
         wait_edge()
         top = slice(base, base + edge)
         low = slice(padded_rows - base - edge, padded_rows - base)
         obj[:, :, top] = obj[:, :, top] - step * (grad[:, :, top] + up[...])
         obj[:, :, low] = obj[:, :, low] - step * (grad[:, :, low] + down[...])
         if final:
-            stores = [
-                pltpu.make_async_copy(
-                    obj.at[:, j, margin : margin + rows],
-                    obj_out.at[:, :, j * length : (j + 1) * length], load_sems.at[j],
-                )
-                for j in range(blocks)
-            ]
-            for store in stores:
-                store.start()
+            loop(groups, lambda g: share_new(fresh, g))
+            energy_to_mate().wait_send()
+            for d in range(1, chips):
+                energy_to(peer(d), d).wait_send()
+            loop(groups, lambda g: finish(fresh, g))
+            loop(groups, lambda g: new_to_mate(fresh, g, 1 - core).wait_recv())
         else:
             clear_outside()
 
-        def share_new(g, carry):
-            for d in range(1, chips):
-                new_from(g, peer(d)).wait_recv()
-            new_to_mate(g, core).start()
-            return carry
-
-        lax.fori_loop(0, groups, share_new, 0)
-
-        def finish(g, carry):
-            grad_to_mate(g).wait_send()
-            for d in range(1, chips):
-                sum_to(g, peer(d), d).wait_send()
-                new_to(g, peer(d), d).wait_send()
-            return carry
-
-        energy_to_mate().wait_send()
-        for d in range(1, chips):
-            energy_to(peer(d), d).wait_send()
-        lax.fori_loop(0, groups, finish, 0)
-        if final:
-            def arrive(g, carry):
-                new_to_mate(g, 1 - core).wait_recv()
-                new_to_mate(g, core).wait_send()
-                return carry
-
-            lax.fori_loop(0, groups, arrive, 0)
-            result = pltpu.make_async_copy(fresh, probe_out, load_sems.at[blocks])
-            result.start()
-            for store in stores:
-                store.wait()
-            result.wait()
+
+def store_kernel(obj, fresh, obj_out, probe_out, sems):
+    blocks, rows, length = obj.shape[1], obj_out.shape[1], obj.shape[3]
+    margin = (obj.shape[2] - rows) // 2
+    copies = [
+        pltpu.make_async_copy(
+            obj.at[:, j, margin : margin + rows],
+            obj_out.at[:, :, j * length : (j + 1) * length], sems.at[j],
+        )
+        for j in range(blocks)
+    ] + [pltpu.make_async_copy(fresh, probe_out, sems.at[blocks])]
+    for copy in copies:
+        copy.start()
+    for copy in copies:
+        copy.wait()
 
 
 def body(object_tile, probe_modes, measured, offsets, counts):
@@ -472,6 +520,7 @@
     padded = rows + 2 * margin
     half = modes * length
     chips = n // 2
+    teams = 1 if slots % 2 else 2
     groups = modes
     while groups > 1 and (modes % groups or half // groups % (chips * SUBLANES)):
         groups -= 1
@@ -483,27 +532,24 @@
     def vmem(*shape, dtype=f32):
         return pltpu.VMEM(shape, dtype)
 
-    new_object, fresh = pl.pallas_call(
-        functools.partial(steps_kernel, n, groups),
+    padded_object, fresh = pl.pallas_call(
+        functools.partial(steps_kernel, n, groups, teams),
         name="steps",
         out_shape=[
-            jax.ShapeDtypeStruct(object_tile.shape, f32),
-            jax.ShapeDtypeStruct((2 * half, length), f32),
+            vmem(2, blocks, padded, length),
+            vmem(2 * half, length),
         ],
         in_specs=[SMEM, SMEM] + [ANY] * 4,
-        out_specs=[ANY] * 2,
+        out_specs=[VMEM] * 2,
         scratch_shapes=[
-            vmem(2, blocks, padded, length),
             vmem(2, blocks, padded, length),
             vmem(max(slots - 2, 1), 2, blocks, 2 * padded - length, length),
             vmem(slots, 2, length, length),
             vmem(modes, slots * length, 2 * length),
-            vmem(4 * length, slots * length, dtype=bf16),
-            vmem(slots * length, 4 * length, dtype=bf16),
             vmem(slots, length, length),
             vmem(slots, length, length),
             vmem(slots, 2, length, length),
-            vmem(ITERS + 1, 2 * half, length),
+            vmem(ITERS, 2 * half, length),
             vmem(2, half, length),
             vmem(half, length),
             vmem(half, length),
@@ -518,13 +564,25 @@
             dma((blocks + 3,)), dma((4,)), dma((ITERS, 4)),
             dma((2,)), dma((chips,)), dma((chips,)),
             dma((4, groups)),
+            pltpu.SemaphoreType.REGULAR((n.bit_length(), 2)),
             dma((groups, chips)), dma((groups, chips)), dma((groups, chips)), dma((groups, chips)),
         ],
         compiler_params=pltpu.CompilerParams(collective_id=0, has_side_effects=True),
     )(
         offsets.T, counts, object_tile, probe_modes.reshape(2 * half, length), measured, tables
     )
-    return (new_object, fresh.reshape(probe_modes.shape))
+    new_object, new_probe = pl.pallas_call(
+        store_kernel,
+        name="store",
+        out_shape=[
+            jax.ShapeDtypeStruct(object_tile.shape, f32),
+            jax.ShapeDtypeStruct((2 * half, length), f32),
+        ],
+        in_specs=[VMEM] * 2,
+        out_specs=[ANY] * 2,
+        scratch_shapes=[dma((blocks + 1,))],
+    )(*[pltpu.with_memory_space_constraint(x, pltpu.VMEM) for x in (padded_object, fresh)])
+    return (new_object, new_probe.reshape(probe_modes.shape))
 
 
 def solution(mesh):

time: 62.3 us -> 57.2 us (0.918)
  local copies, waits for them, and re-layouts: 2.72 us -> 0 us
  Pallas kernels: 58.1 us -> 55.8 us
    unnamed x4 -> x0, local copies, waits for them, and re-layouts: 2.72 us -> none
    pallas_call x1 -> x2, Pallas kernels: 58.1 us -> 55.8 us  [the longest x1 54.8 us: body(): pl.pallas_call(functools.partial(steps_kernel, n, groups, teams), name='s...]
where the time goes in v2:
time: 57.2 us; the launch traced here: 57.1 us
  Pallas kernels  55.8 us (98%)
  between operations  1.29 us (2%)
    pallas_call x1, Pallas kernels, body(): pl.pallas_call(functools.partial(steps_kernel, n, groups, teams), name='s...  54.8 us

profile of v2, /device:TPU:0, one launch (start us, length us, event | category | flops | bytes accessed | tf_op | source)
XLA Modules:
  0.0 57.1 jit_solution(11347596553208074419)
XLA Ops:
  1.3 54.8 %steps.1 = (f32[2,2,384,128]{3,2,1,0:T(8,128)S(1)}, f32[1024,128]{1,0:T(8,128)S(1)}) custom-call(s32[2,4]{1,0:T(2,128)} %bitcast.4, s32[1]{0:T(128)S(6)} %copy.8.counts, f32[2,256,256]{2,1,0:T(8,128)} %tile.1, f32[1024,128]{1,0:T(8,128)} %bitcast.3, f32[4,128,128]{2,1,0:T(8,128)} %measured_in.1, bf16[4,256,256]{2,1,0:T(8,128)(2,1)} %constant.2.clone.tables_in), custom_call_target="tpu_custom_call" | custom-call | tf_op jit(solution)/shard_map/steps/pallas_call | solution.py:535
  56.1 1.0 %store.1 = (f32[2,256,256]{2,1,0:T(8,128)}, f32[1024,128]{1,0:T(8,128)}) custom-call(f32[2,2,384,128]{3,2,1,0:T(8,128)S(1)} %get-tuple-element.6.obj, f32[1024,128]{1,0:T(8,128)S(1)} %get-tuple-element.7.fresh), custom_call_target="tpu_custom_call" | custom-call | tf_op jit(solution)/shard_map/store/pallas_call | solution.py:574

commit v3 on v2

--- a/solution.py
+++ b/solution.py
@@ -340,7 +340,11 @@
 
         if sweep:
             share_new(probe, 0)
-        loop(groups, forward_group)
+        if sweep:
+            loop(groups, forward_group)
+        else:
+            for g in range(groups):
+                forward_group(g)
         if sweep:
             loop(groups, lambda g: finish(probe, g))
 

time: 57.2 us -> 56.7 us (level)
  Pallas kernels: 55.8 us -> 55.2 us
where the time goes in v3:
time: 56.7 us; the launch traced here: 56.5 us
  Pallas kernels  55.2 us (97%)
  between operations  1.29 us (2%)
    pallas_call x1, Pallas kernels, body(): pl.pallas_call(functools.partial(steps_kernel, n, groups, teams), name='s...  54.2 us

profile of v3, /device:TPU:0, one launch (start us, length us, event | category | flops | bytes accessed | tf_op | source)
XLA Modules:
  0.0 56.5 jit_solution(8335984125045929497)
XLA Ops:
  1.3 54.2 %steps.1 = (f32[2,2,384,128]{3,2,1,0:T(8,128)S(1)}, f32[1024,128]{1,0:T(8,128)S(1)}) custom-call(s32[2,4]{1,0:T(2,128)} %bitcast.4, s32[1]{0:T(128)S(6)} %copy.8.counts, f32[2,256,256]{2,1,0:T(8,128)} %tile.1, f32[1024,128]{1,0:T(8,128)} %bitcast.3, f32[4,128,128]{2,1,0:T(8,128)} %measured_in.1, bf16[4,256,256]{2,1,0:T(8,128)(2,1)} %constant.2.clone.tables_in), custom_call_target="tpu_custom_call" | custom-call | tf_op jit(solution)/shard_map/steps/pallas_call | solution.py:539
  55.5 1.0 %store.1 = (f32[2,256,256]{2,1,0:T(8,128)}, f32[1024,128]{1,0:T(8,128)}) custom-call(f32[2,2,384,128]{3,2,1,0:T(8,128)S(1)} %get-tuple-element.6.obj, f32[1024,128]{1,0:T(8,128)S(1)} %get-tuple-element.7.fresh), custom_call_target="tpu_custom_call" | custom-call | tf_op jit(solution)/shard_map/store/pallas_call | solution.py:578
